TPU v7x, 32 devices: a whole 2x2x4 slice. The times are simulated.
32 devices in a mesh: tm: 8 (over z, x), space: 4 (over y, core).
Axes of the slice: x: 2, y: 2, z: 4, core: 2. Of those that a mesh axis runs over, the one named last changes fastest.
Arguments:
- u_old: float32 [8, 5, 256, 16, 128], P('tm', None, 'space'), may hold values from -2.5 to 2.5
- u_init: float32 [256, 16, 128], P('space'), may hold values from -2.5 to 2.5
Outputs:
- u_new: float32 [8, 5, 256, 16, 128], P('tm', None, 'space')
All inputs are finite; a program needn't handle non-finite values.
Results may differ from a plain program's by a relative error of at most 0.0003.
Values sent between devices are 32-bit elements; how exact they have to be, the bound alone decides.
A program may use at most 128 MiB of HBM per device.

v0:
```python
import math

import jax
import jax.numpy as jnp
from jax import lax
from jax.sharding import PartitionSpec as P

step_length = 0.4
diffusion = 1.0
reaction = 1.0


def padded_2(x, sides, width):
    for axis, dim in sides:
        count, length = (lax.axis_size(axis), x.shape[dim])
        up = [(i, (i + 1) % count) for i in range(count)]
        down = [(j, i) for i, j in up]
        last = lax.slice_in_dim(x, length - width, length, axis=dim)
        leading = lax.slice_in_dim(x, 0, width, axis=dim)
        before = lax.ppermute(last, axis, up)
        after = lax.ppermute(leading, axis, down)
        x = jnp.concatenate([before, x, after], axis=dim)
    return x


def passed_along(value, axis, steps):
    count = lax.axis_size(axis)
    leading, last = (max(0, -steps), min(count, count - steps))
    return lax.ppermute(value, axis, [(source, source + steps) for source in range(leading, last)])


def entering(part, axis, combine, identity):
    place = lax.axis_index(axis)
    gathered = jax.tree.map(lambda a: lax.all_gather(a, axis), part)
    state = jax.tree.map(lambda a, e: jnp.zeros_like(a) + jnp.asarray(e, a.dtype), part, identity)

    def one(hop, state):
        return combine(
            state, jax.tree.map(lambda a: lax.dynamic_index_in_dim(a, hop, 0, False), gathered)
        )

    return lax.fori_loop(0, place, one, state)


def basis_coefficients(nodes, chosen):
    polynomial = [1.0]
    for other, point in enumerate(nodes):
        if other == chosen:
            continue
        divisor = nodes[chosen] - point
        widened = [0.0] * (len(polynomial) + 1)
        for power, value in enumerate(polynomial):
            widened[power + 1] += value / divisor
            widened[power] -= value * point / divisor
        polynomial = widened
    return polynomial


def basis_value(nodes, chosen, where):
    result = 1.0
    for other, point in enumerate(nodes):
        if other != chosen:
            result *= (where - point) / (nodes[chosen] - point)
    return result


def node_tables():
    root = math.sqrt(3.0 / 7.0)
    fine_tau = [0.0, (1.0 - root) / 2.0, 0.5, (1.0 + root) / 2.0, 1.0]
    coarse_tau = [0.0, 0.5, 1.0]
    integ = []
    for j in range(4):
        row_values = []
        for k in range(5):
            polynomial = basis_coefficients(fine_tau, k)
            total = 0.0
            for power, value in enumerate(polynomial):
                total += (
                    value
                    * (fine_tau[j + 1] ** (power + 1) - fine_tau[j] ** (power + 1))
                    / (power + 1)
                )
            row_values.append(total)
        integ.append(row_values)
    interp = [[basis_value(coarse_tau, c, fine_tau[m]) for c in range(3)] for m in range(5)]
    spacing = [float(fine_tau[j + 1] - fine_tau[j]) for j in range(4)]
    return (jnp.asarray(integ, jnp.float32), spacing, jnp.asarray(interp, jnp.float32))


def hartley(length):
    counter = jnp.arange(length, dtype=jnp.int32)
    product = counter[:, None] * counter[None, :] % length
    phase = 2.0 * jnp.pi * product.astype(jnp.float32) / length
    return (jnp.cos(phase) + jnp.sin(phase)) / math.sqrt(length)


def local_force(padded):
    field = padded[:, 1:-1]
    near = padded[:, 2:] + padded[:, :-2] + jnp.roll(field, 1, 2) + jnp.roll(field, -1, 2)
    near = near + jnp.roll(field, 1, 3) + jnp.roll(field, -1, 3)
    return diffusion * (near - 6.0 * field) + reaction * (field - field * field * field)


def fine_force(field):
    padded = padded_2(field, (("space", 1),), 1)
    return local_force(padded)


def restrict(field):
    depth, rows, cols = field.shape
    return (
        field.reshape(depth // 2, 2, rows // 2, 2, cols // 2, 2)
        .mean(axis=(1, 3, 5))
        .reshape(depth // 2, rows * cols // 4)
    )


def compose(earlier, later):
    return (later[0] * earlier[0], later[0] * earlier[1] + later[1])


def shards(u_old, u_init):
    integ, spacing, interp = node_tables()
    highest = lax.Precision.HIGHEST
    depth, rows, cols = u_init.shape
    fine_old = u_old[0]
    previous = passed_along(fine_old[4], "tm", 1)
    position = lax.axis_index("tm")
    start = jnp.where(position == 0, u_init, previous)
    states = [start]
    forces = []
    fold = fine_force(fine_old)
    iold = step_length * jnp.einsum("jk,kzxy->jzxy", integ, fold, precision=highest)
    for section in range(4):
        force_now = fine_force(states[section][None])[0]
        forces.append(force_now)
        states.append(
            states[section]
            + step_length * spacing[section] * (force_now - fold[section])
            + iold[section]
        )
    forces.append(fine_force(states[4][None])[0])
    inew = step_length * jnp.einsum("jk,kzxy->jzxy", integ, jnp.stack(forces), precision=highest)
    stacked = jnp.stack(
        [
            restrict(states[0]),
            restrict(states[2]),
            restrict(states[4]),
            restrict(inew[0] + inew[1]),
            restrict(inew[2] + inew[3]),
            restrict(u_init),
        ]
    )
    planes_c = depth // 2
    rows_c = rows // 2
    cols_c = cols // 2
    depth_c = planes_c * lax.axis_size("space")
    table_xy = jnp.kron(hartley(rows_c), hartley(cols_c))
    table_z = hartley(depth_c)
    spectral_xy = jnp.einsum("fzc,cd->fzd", stacked, table_xy, precision=highest)
    wave_z = jnp.arange(depth_c, dtype=jnp.int32)
    wave_xy = jnp.arange(rows_c * cols_c, dtype=jnp.int32)
    angle_z = 2.0 * jnp.cos(2.0 * jnp.pi * wave_z.astype(jnp.float32) / depth_c)
    angle_x = 2.0 * jnp.cos(2.0 * jnp.pi * (wave_xy // cols_c).astype(jnp.float32) / rows_c)
    angle_y = 2.0 * jnp.cos(2.0 * jnp.pi * (wave_xy % cols_c).astype(jnp.float32) / cols_c)
    eigen_all = 0.25 * (angle_z[:, None] + angle_x[None, :] + angle_y[None, :] - 6.0)
    place = lax.axis_index("space")
    columns = lax.all_to_all(spectral_xy, "space", split_axis=2, concat_axis=1, tiled=True)
    spectra = jnp.einsum("qz,fzc->fqc", table_z, columns, precision=highest)
    width = columns.shape[2]
    eigen = lax.dynamic_slice_in_dim(eigen_all, place * width, width, 1)
    pieces = [spectra[k] for k in range(6)]
    damping = 0.5 * step_length * diffusion * eigen
    denom = 1.0 - damping
    lifted0 = pieces[3] - damping * pieces[1]
    lifted1 = pieces[4] - damping * pieces[2]
    slope = 1.0 / (denom * denom)
    offset = (lifted0 / denom + lifted1) / denom
    before_slope, before_offset = entering(
        (slope, offset), "tm", compose, (jnp.ones_like(slope), jnp.zeros_like(offset))
    )
    begin = before_slope * pieces[5] + before_offset
    middle = (begin + lifted0) / denom
    finish = (middle + lifted1) / denom
    delta = jnp.stack([begin - pieces[0], middle - pieces[1], finish - pieces[2]])
    planar = jnp.einsum("zq,fqc->fzc", table_z, delta, precision=highest)
    returned = lax.all_to_all(planar, "space", split_axis=1, concat_axis=2, tiled=True)
    real_space = jnp.einsum("fzc,cd->fzd", returned, table_xy, precision=highest)
    coarse_grid = real_space.reshape(3, planes_c, rows_c, cols_c)
    timed = jnp.einsum("mc,czxy->mzxy", interp, coarse_grid, precision=highest)
    upper = jnp.repeat(jnp.repeat(jnp.repeat(timed, 2, 1), 2, 2), 2, 3)
    return (jnp.stack(states) + upper)[None]


def solution(mesh):
    return jax.shard_map(
        shards,
        mesh=mesh,
        in_specs=(P("tm", None, "space", None, None), P("space", None, None)),
        out_specs=P("tm", None, "space", None, None),
        check_vma=False,
    )
```

profile of v0, /device:TPU:25, one launch (start us, length us, event | category | flops | bytes accessed | tf_op | source)
XLA Modules:
  0.0 488.8 jit_solution(6314693556125100322)
XLA Ops:
  8.6 5.6 %fusion.146 = (f32[5,64,16,127]{3,2,1,0:T(8,128)}, f32[5,64,16,127]{3,2,1,0:T(8,128)}) fusion(f32[5,64,16,128]{3,2,1,0:T(8,128)} %bitcast.222), kind=kLoop, calls=%fused_computation.218 | loop fusion | bytes 10403840 | tf_op jit(solution)/shard_map/jit(_roll_static)/slice | solution.py:100
  20.6 35.2 %reshape.320 = f32[32,2,8,2,64,2]{5,4,3,2,1,0:T(8,128)} reshape(f32[64,16,128]{2,1,0:T(8,128)S(1)} %copy-done.6) | data formatting | bytes 1048576 | tf_op jit(solution)/shard_map/reshape | solution.py:112
  55.8 12.9 %reduce_sum.59 = f32[32,8,64]{2,1,0:T(8,128)} reduce(f32[32,2,8,2,64,2]{5,4,3,2,1,0:T(8,128)} %reshape.320, f32[]{:T(128)} %constant.137.clone.1), dimensions={1,3,5}, to_apply=%region_5.6 | reduce | flops 114688 | bytes 589828 | tf_op jit(solution)/shard_map/reduce_sum | solution.py:113
  75.6 7.2 %fusion.4 = f32[5,64,16,128]{3,2,1,0:T(8,128)S(1)} fusion(f32[5,64,16,128]{3,2,1,0:T(8,128)S(1)} %bitcast.226, f32[5,1,16,128]{3,2,1,0:T(8,128)} %collective-permute-done.4, f32[5,1,16,128]{3,2,1,0:T(8,128)} %collective-permute-done.3, f32[5,64,15,128]{3,2,1,0:T(8,128)} %get-tuple-element.112, f32[5,64,1,128]{3,2,1,0:T(1,128)S(1)} %get-tuple-element.114, ...), kind=kLoop, calls=%fused_computation.8 | loop fusion | flops 11141120 | bytes 15810560 | tf_op jit(solution)/shard_map/add | solution.py:101
  82.7 5.5 %multiply_bitcast_fusion.1 = f32[4,64,16,128]{3,0,2,1:T(4,128)S(1)} fusion(f32[4,5,1,1]{1,0,3,2:T(4,128)S(1)} %copy-done.11, f32[5,64,16,128]{3,2,1,0:T(8,128)S(1)} %fusion.4), kind=kOutput, calls=%fused_computation.18 | convolution fusion | flops 31981568 | bytes 4718672 | tf_op jit(solution)/shard_map/jk,kzxy->jzxy/dot_general | solution.py:133
  96.3 34.9 %reshape.317 = f32[32,2,8,2,64,2]{5,4,3,2,1,0:T(8,128)} reshape(f32[64,16,128]{2,1,0:T(8,128)S(1)} %get-tuple-element.104) | data formatting | bytes 1048576 | tf_op jit(solution)/shard_map/reshape | solution.py:112
  132.9 12.7 %reduce_sum.54 = f32[32,8,64]{2,1,0:T(8,128)S(1)} reduce(f32[32,2,8,2,64,2]{5,4,3,2,1,0:T(8,128)} %reshape.317, f32[]{:T(128)} %constant.137.clone.1), dimensions={1,3,5}, to_apply=%region_0.1 | reduce | flops 114688 | bytes 589828 | tf_op jit(solution)/shard_map/reduce_sum | solution.py:113
  160.5 34.9 %reshape.318 = f32[32,2,8,2,64,2]{5,4,3,2,1,0:T(8,128)} reshape(f32[64,16,128]{2,1,0:T(8,128)S(1)} %get-tuple-element.100) | data formatting | bytes 1048576 | tf_op jit(solution)/shard_map/reshape | solution.py:112
  197.1 12.2 %reduce_sum.55 = f32[32,8,64]{2,1,0:T(8,128)S(1)} reduce(f32[32,2,8,2,64,2]{5,4,3,2,1,0:T(8,128)} %reshape.318, f32[]{:T(128)} %constant.137.clone.1), dimensions={1,3,5}, to_apply=%region_1.2 | reduce | flops 114688 | bytes 589828 | tf_op jit(solution)/shard_map/reduce_sum | solution.py:113
  225.2 34.9 %reshape.319 = f32[32,2,8,2,64,2]{5,4,3,2,1,0:T(8,128)} reshape(f32[64,16,128]{2,1,0:T(8,128)S(1)} %get-tuple-element.96) | data formatting | bytes 1048576 | tf_op jit(solution)/shard_map/reshape | solution.py:112
  261.8 12.4 %reduce_sum.56 = f32[32,8,64]{2,1,0:T(8,128)S(1)} reduce(f32[32,2,8,2,64,2]{5,4,3,2,1,0:T(8,128)} %reshape.319, f32[]{:T(128)} %constant.137.clone.1), dimensions={1,3,5}, to_apply=%region_2.3 | reduce | flops 114688 | bytes 589828 | tf_op jit(solution)/shard_map/reduce_sum | solution.py:113
  277.3 5.5 %multiply_bitcast_fusion = f32[4,64,16,128]{3,0,2,1:T(4,128)S(1)} fusion(f32[4,5,1,1]{1,0,3,2:T(4,128)S(1)} %copy-done.12, f32[5,64,16,128]{3,2,1,0:T(8,128)S(1)} %fusion.27), kind=kOutput, calls=%fused_computation.17 | convolution fusion | flops 31981568 | bytes 4718672 | tf_op jit(solution)/shard_map/jk,kzxy->jzxy/dot_general | solution.py:143
  282.8 3.5 fusion.28
  286.3 34.9 %add.334 = f32[32,2,8,2,64,2]{5,4,3,2,1,0:T(8,128)} reshape(f32[64,16,128]{2,1,0:T(8,128)S(1)} %get-tuple-element.72) | data formatting | bytes 1048576 | tf_op jit(solution)/shard_map/add | solution.py:149
  321.2 12.2 %reduce_sum.57 = f32[32,8,64]{2,1,0:T(8,128)S(1)} reduce(f32[32,2,8,2,64,2]{5,4,3,2,1,0:T(8,128)} %add.334, f32[]{:T(128)} %constant.137.clone.1), dimensions={1,3,5}, to_apply=%region_3.4 | reduce | flops 114688 | bytes 589828 | tf_op jit(solution)/shard_map/reduce_sum | solution.py:113
  333.5 34.9 %add.336 = f32[32,2,8,2,64,2]{5,4,3,2,1,0:T(8,128)} reshape(f32[64,16,128]{2,1,0:T(8,128)S(1)} %get-tuple-element.71) | data formatting | bytes 1048576 | tf_op jit(solution)/shard_map/add | solution.py:150
  368.4 12.3 %reduce_sum.58 = f32[32,8,64]{2,1,0:T(8,128)S(1)} reduce(f32[32,2,8,2,64,2]{5,4,3,2,1,0:T(8,128)} %add.336, f32[]{:T(128)} %constant.137.clone.1), dimensions={1,3,5}, to_apply=%region_4.5 | reduce | flops 114688 | bytes 589828 | tf_op jit(solution)/shard_map/reduce_sum | solution.py:113
  387.1 3.7 all-to-all-start
  391.1 5.8 %all-to-all-done = f32[4,1,24576]{2,1,0:T(1,128)S(1)} async-done(((f32[4,1,24576]{2,1,0:T(1,128)}), f32[4,1,24576]{2,1,0:T(1,128)S(1)}, u32[]{:S(2)}, u32[]{:S(2)}) %all-to-all-start) | async-done | bytes 393248 | tf_op jit(solution)/shard_map/all_to_all | solution.py:168
  401.7 22.9 %all-gather = f32[1024,128]{0,1:T(8,128)S(1)} all-gather(f32[128,128]{0,1:T(8,128)S(1)} %get-tuple-element.173), channel_id=2, replica_groups=mesh['tm'=8,'space'=4] {'tm'}, dimensions={0}, use_global_device_ids=true | all-gather | bytes 589824 | tf_op jit(solution)/shard_map/all_gather | solution.py:34
  424.8 25.4 %all-gather.1 = f32[1024,128]{0,1:T(8,128)S(1)} all-gather(f32[128,128]{0,1:T(8,128)S(1)} %get-tuple-element.172), channel_id=3, replica_groups=mesh['tm'=8,'space'=4] {'tm'}, dimensions={0}, use_global_device_ids=true | all-gather | bytes 589824 | tf_op jit(solution)/shard_map/all_gather | solution.py:34
  452.0 20.3 %all_to_all.36 = f32[3,128,128]{2,0,1:T(4,128)S(1)} all-to-all(f32[3,128,128]{2,0,1:T(4,128)S(1)} %copy.88), channel_id=1, replica_groups=mesh['tm'=8,'space'=4] {'space'}, dimensions={1} | all-to-all | bytes 393216 | tf_op jit(solution)/shard_map/all_to_all | solution.py:187
  480.1 4.9 copy.94
  485.0 3.6 add.347
  (159 shorter events, 90.4 us)
Async XLA Ops:
  1.9 89.2 %collective-permute-start = (f32[64,16,128]{2,1,0:T(8,128)}, f32[64,16,128]{2,1,0:T(8,128)}, u32[]{:S(2)}, u32[]{:S(2)}) collective-permute-start(f32[64,16,128]{2,1,0:T(8,128)} %slice_bitcast_fusion), channel_id=1, source_target_pairs={{0,4},{4,8},{8,12},{12,16},{16,20},{20,24},{24,28},{1,5},{5,9},{9,... | collective-permute-start | bytes 1572872 | tf_op jit(solution)/shard_map/ppermute | solution.py:29
  6.4 69.1 %collective-permute-start.3 = (f32[5,1,16,128]{3,2,1,0:T(8,128)}, f32[5,1,16,128]{3,2,1,0:T(8,128)}, u32[]{:S(2)}, u32[]{:S(2)}) collective-permute-start(f32[5,1,16,128]{3,2,1,0:T(8,128)} %get-tuple-element.115), channel_id=1, source_target_pairs={{1,0},{2,1},{3,2},{0,3},{5,4},{6,5},{7,6},{4,7},{9,8},{10,9},{11,1... | collective-permute-start | bytes 122888 | tf_op jit(solution)/shard_map/ppermute | solution.py:21
  7.4 6.8 %copy-start = (f32[1,5,64,16,128]{4,3,2,1,0:T(8,128)S(1)}, f32[1,5,64,16,128]{4,3,2,1,0:T(8,128)}, u32[]{:S(2)}) copy-start(f32[1,5,64,16,128]{4,3,2,1,0:T(8,128)} %param.6) | copy-start | bytes 7864324
  7.4 68.2 %collective-permute-start.4 = (f32[5,1,16,128]{3,2,1,0:T(8,128)}, f32[5,1,16,128]{3,2,1,0:T(8,128)}, u32[]{:S(2)}, u32[]{:S(2)}) collective-permute-start(f32[5,1,16,128]{3,2,1,0:T(8,128)} %get-tuple-element.116), channel_id=1, source_target_pairs={{0,1},{1,2},{2,3},{3,0},{4,5},{5,6},{6,7},{7,4},{8,9},{9,10},{10,1... | collective-permute-start | bytes 122888 | tf_op jit(solution)/shard_map/ppermute | solution.py:20
  17.4 3.3 copy-start.6
  75.5 7.2 %copy-start.11 = (f32[4,5,1,1]{1,0,3,2:T(4,128)S(1)}, f32[4,5,1,1]{1,0,3,2:T(4,128)}, u32[]{:S(2)}) copy-start(f32[4,5,1,1]{1,0,3,2:T(4,128)} %constant.162) | copy-start | bytes 244
  82.7 5.5 %copy-start.1 = (f32[5,64,16,128]{3,2,1,0:T(8,128)}, f32[5,64,16,128]{3,2,1,0:T(8,128)S(1)}, u32[]{:S(2)}) copy-start(f32[5,64,16,128]{3,2,1,0:T(8,128)S(1)} %fusion.4) | copy-start | bytes 7864324
  131.2 15.2 %collective-permute-start.1 = (f32[1,1,16,128]{3,2,1,0:T(8,128)S(1)}, f32[1,1,16,128]{3,2,1,0:T(8,128)S(1)}, u32[]{:S(2)}, u32[]{:S(2)}) collective-permute-start(f32[1,1,16,128]{3,2,1,0:T(8,128)S(1)} %get-tuple-element.162), channel_id=1, source_target_pairs={{1,0},{2,1},{3,2},{0,3},{5,4},{6,5},{7,6},{4,7},{9,8},{10,9},{11,1... | collective-permute-start | bytes 24584 | tf_op jit(solution)/shard_map/ppermute | solution.py:21
  131.2 15.2 %collective-permute-start.2 = (f32[1,1,16,128]{3,2,1,0:T(8,128)S(1)}, f32[1,1,16,128]{3,2,1,0:T(8,128)S(1)}, u32[]{:S(2)}, u32[]{:S(2)}) collective-permute-start(f32[1,1,16,128]{3,2,1,0:T(8,128)S(1)} %get-tuple-element.163), channel_id=1, source_target_pairs={{0,1},{1,2},{2,3},{3,0},{4,5},{5,6},{6,7},{7,4},{8,9},{9,10},{10,1... | collective-permute-start | bytes 24584 | tf_op jit(solution)/shard_map/ppermute | solution.py:20
  146.4 2.8 copy-start.10
  150.7 3.1 collective-permute-start.5
  150.8 3.1 collective-permute-start.6
  195.4 14.7 %collective-permute-start.7 = (f32[1,1,16,128]{3,2,1,0:T(8,128)}, f32[1,1,16,128]{3,2,1,0:T(8,128)S(1)}, u32[]{:S(2)}, u32[]{:S(2)}) collective-permute-start(f32[1,1,16,128]{3,2,1,0:T(8,128)} %get-tuple-element.142), channel_id=1, source_target_pairs={{1,0},{2,1},{3,2},{0,3},{5,4},{6,5},{7,6},{4,7},{9,8},{10,9},{11,1... | collective-permute-start | bytes 24584 | tf_op jit(solution)/shard_map/ppermute | solution.py:21
  196.6 13.5 %collective-permute-start.8 = (f32[1,1,16,128]{3,2,1,0:T(8,128)}, f32[1,1,16,128]{3,2,1,0:T(8,128)S(1)}, u32[]{:S(2)}, u32[]{:S(2)}) collective-permute-start(f32[1,1,16,128]{3,2,1,0:T(8,128)} %get-tuple-element.143), channel_id=1, source_target_pairs={{0,1},{1,2},{2,3},{3,0},{4,5},{5,6},{6,7},{7,4},{8,9},{9,10},{10,1... | collective-permute-start | bytes 24584 | tf_op jit(solution)/shard_map/ppermute | solution.py:20
  210.1 3.2 copy-start.8
  214.7 1.4 collective-permute-start.10
  215.3 3.1 collective-permute-start.9
  260.1 14.9 %collective-permute-start.11 = (f32[1,1,16,128]{3,2,1,0:T(8,128)}, f32[1,1,16,128]{3,2,1,0:T(8,128)S(1)}, u32[]{:S(2)}, u32[]{:S(2)}) collective-permute-start(f32[1,1,16,128]{3,2,1,0:T(8,128)} %get-tuple-element.130), channel_id=1, source_target_pairs={{1,0},{2,1},{3,2},{0,3},{5,4},{6,5},{7,6},{4,7},{9,8},{10,9},{11,1... | collective-permute-start | bytes 24584 | tf_op jit(solution)/shard_map/ppermute | solution.py:21
  260.1 14.9 %copy-start.5 = (f32[5,64,16,128]{3,2,1,0:T(8,128)S(1)}, f32[5,64,16,128]{3,2,1,0:T(8,128)}, u32[]{:S(2)}) copy-start(f32[5,64,16,128]{3,2,1,0:T(8,128)} %get-tuple-element.87) | copy-start | bytes 7864324
  260.1 14.9 %collective-permute-start.12 = (f32[1,1,16,128]{3,2,1,0:T(8,128)}, f32[1,1,16,128]{3,2,1,0:T(8,128)S(1)}, u32[]{:S(2)}, u32[]{:S(2)}) collective-permute-start(f32[1,1,16,128]{3,2,1,0:T(8,128)} %get-tuple-element.131), channel_id=1, source_target_pairs={{0,1},{1,2},{2,3},{3,0},{4,5},{5,6},{6,7},{7,4},{8,9},{9,10},{10,1... | collective-permute-start | bytes 24584 | tf_op jit(solution)/shard_map/ppermute | solution.py:20
  274.2 3.1 copy-start.12
  368.4 14.3 %copy-start.3 = (f32[512,512]{0,1:T(8,128)S(1)}, f32[512,512]{0,1:T(8,128)}, u32[]{:S(2)}) copy-start(f32[512,512]{0,1:T(8,128)} %mul.340) | copy-start | bytes 3145732
  387.1 9.7 %all-to-all-start = ((f32[4,1,24576]{2,1,0:T(1,128)}), f32[4,1,24576]{2,1,0:T(1,128)S(1)}, u32[]{:S(2)}, u32[]{:S(2)}) async-start(f32[4,1,24576]{2,1,0:T(1,128)} %reshape.345), calls=%async_computation | async-start | bytes 786432 | tf_op jit(solution)/shard_map/all_to_all | solution.py:168
  451.0 23.2 %copy-start.13 = (f32[5,3,1,1]{0,1,3,2:T(4,128)S(1)}, f32[5,3,1,1]{0,1,3,2:T(4,128)}, u32[]{:S(2)}) copy-start(f32[5,3,1,1]{0,1,3,2:T(4,128)} %constant.163) | copy-start | bytes 184
  (4 other events, 7.8 us)
where the time goes:
time: 497 us; the launch traced here: 489 us
  local copies, waits for them, and re-layouts  264 us (53%)
  other arithmetic  111 us (22%)
  blocking collectives  68.6 us (14%)
  matrix products  17.7 us (4%)
  starting transfers between devices  16.5 us (3%)
  waiting for transfers between devices  10.1 us (2%)
    reshape x4, local copies, waits for them, and re-layouts, restrict(): field.reshape(depth // 2, 2, rows // 2, 2, cols // 2, 2)  140 us
    reduce_sum x6, other arithmetic, restrict(): return field.reshape(depth // 2, 2, rows // 2, 2, cols // 2, 2).mean(axis...  74.7 us
    all_gather x2, blocking collectives, entering(): gathered = jax.tree.map(lambda a: lax.all_gather(a, axis), part)  48.3 us
    add x1, local copies, waits for them, and re-layouts, shards(): inew[0] + inew[1]  34.9 us
    add x1, local copies, waits for them, and re-layouts, shards(): inew[2] + inew[3]  34.9 us
    all_to_all x1, blocking collectives, shards(): lax.all_to_all(planar, 'space', split_axis=1, concat_axis=2, tiled=True)  20.3 us
    slice x12, local copies, waits for them, and re-layouts, local_force(): near = near + jnp.roll(field, 1, 3) + jnp.roll(field, -1, 3)  16.2 us
    unnamed x8, other arithmetic  12.5 us
  transfers between devices with their start and end apart: 14, of which 4 were waited for; matrix products, arithmetic and copies ran while one was open for 25% of the time, Pallas kernels for 0%

commit v1 on v0

v1 whole, which is shorter than its diff:
```python
import functools
import math

import jax
import jax.numpy as jnp
import numpy as np
from jax import lax
from jax.experimental import pallas as pl
from jax.experimental.pallas import tpu as pltpu
from jax.sharding import PartitionSpec as P

step_length = 0.4
diffusion = 1.0
reaction = 1.0
HALO = 5
BLOCK = 4
MESH = pl.DeviceIdType.MESH


def basis_coefficients(nodes, chosen):
    polynomial = [1.0]
    for other, point in enumerate(nodes):
        if other == chosen:
            continue
        divisor = nodes[chosen] - point
        widened = [0.0] * (len(polynomial) + 1)
        for power, value in enumerate(polynomial):
            widened[power + 1] += value / divisor
            widened[power] -= value * point / divisor
        polynomial = widened
    return polynomial


def basis_value(nodes, chosen, where):
    result = 1.0
    for other, point in enumerate(nodes):
        if other != chosen:
            result *= (where - point) / (nodes[chosen] - point)
    return result


def node_tables():
    root = math.sqrt(3.0 / 7.0)
    fine_tau = [0.0, (1.0 - root) / 2.0, 0.5, (1.0 + root) / 2.0, 1.0]
    coarse_tau = [0.0, 0.5, 1.0]
    integ = []
    for j in range(4):
        row_values = []
        for k in range(5):
            polynomial = basis_coefficients(fine_tau, k)
            total = 0.0
            for power, value in enumerate(polynomial):
                total += (
                    value
                    * (fine_tau[j + 1] ** (power + 1) - fine_tau[j] ** (power + 1))
                    / (power + 1)
                )
            row_values.append(total)
        integ.append(row_values)
    interp = [[basis_value(coarse_tau, c, fine_tau[m]) for c in range(3)] for m in range(5)]
    spacing = [float(fine_tau[j + 1] - fine_tau[j]) for j in range(4)]
    return integ, spacing, interp


def hartley(length):
    counter = np.arange(length)
    phase = 2.0 * np.pi * (counter[:, None] * counter[None, :] % length) / length
    return (np.cos(phase) + np.sin(phase)) / math.sqrt(length)


def two_parts(table):
    upper = table.astype(jnp.bfloat16)
    lower = (table - upper.astype(np.float64)).astype(jnp.bfloat16)
    return np.stack([upper, lower])


def halves(value):
    upper = value.astype(jnp.bfloat16)
    return upper, (value - upper.astype(jnp.float32)).astype(jnp.bfloat16)


def product(a, b, dims):
    def one(x, y):
        return lax.dot_general(x, y, (dims, ((), ())), preferred_element_type=jnp.float32)

    return one(a[0], b[0]) + (one(a[0], b[1]) + one(a[1], b[0]))


def force(padded):
    field = padded[1:-1]
    rows, cols = field.shape[1:]
    near = padded[2:] + padded[:-2]
    near = near + (pltpu.roll(field, 1, 1) + pltpu.roll(field, rows - 1, 1))
    near = near + (pltpu.roll(field, 1, 2) + pltpu.roll(field, cols - 1, 2))
    linear = reaction - 6.0 * diffusion
    return diffusion * near + field * (linear - reaction * (field * field))


def kernel(
    nt, ns, solvers,
    u_hbm, init_hbm, tab_hbm, ztab_hbm, inv_hbm,
    w_out, timed_out,
    u, w, corr, acc, restricted, tab, ztab, inv,
    send_1, recv_1, send_2, recv_2, up,
    load_sem, table_sem, out_sem, start_sem, halo_send, halo_recv, start_send, start_recv,
    sems,
):
    integ, spacing, interp = node_tables()
    h = step_length
    devices = nt * ns
    depth, rows, cols = init_hbm.shape
    depth_c, rows_c = depth // 2, rows // 2
    length = send_1.shape[2]
    modes = send_1.shape[1]
    own = pl.ds(HALO, depth)
    t, s = lax.axis_index("tm"), lax.axis_index("space")
    me = t * ns + s
    above, below = lax.rem(s + 1, ns), lax.rem(s + ns - 1, ns)

    barrier = pltpu.get_barrier_semaphore()

    def greet(i, carry):
        other = lax.rem(me + i, devices)
        pl.semaphore_signal(
            barrier, inc=1, device_id=(other // ns, lax.rem(other, ns)), device_id_type=MESH
        )
        return carry

    lax.fori_loop(1, devices, greet, 0)
    load = pltpu.make_async_copy(u_hbm.at[0], u.at[:, own], load_sem)
    load.start()
    tables = [
        pltpu.make_async_copy(source, target, table_sem.at[i])
        for i, (source, target) in enumerate(((tab_hbm, tab), (ztab_hbm, ztab), (inv_hbm, inv)))
    ]
    for copy in tables:
        copy.start()
    local_start = pltpu.make_async_copy(init_hbm, w.at[0, own], start_sem)

    @pl.when(t == 0)
    def _():
        local_start.start()

    pl.semaphore_wait(barrier, devices - 1)

    lows, highs = pl.ds(0, HALO), pl.ds(HALO + depth, HALO)
    first, last = pl.ds(0, HALO), pl.ds(depth - HALO, HALO)

    def remote(source, target, send, recv, place):
        return pltpu.make_async_remote_copy(
            src_ref=source, dst_ref=target, send_sem=send, recv_sem=recv,
            device_id=place, device_id_type=MESH,
        )

    after = jnp.minimum(t + 1, nt - 1)
    node = u_hbm.at[0, 4]
    starts = [
        remote(node, w.at[0, own], start_send.at[0], start_recv.at[0], (after, s)),
        remote(node.at[last], w.at[0, lows], start_send.at[1], start_recv.at[1], (after, above)),
        remote(node.at[first], w.at[0, highs], start_send.at[2], start_recv.at[2], (after, below)),
    ]
    inits = [
        remote(init_hbm.at[last], w.at[0, lows], start_send.at[3], start_recv.at[1], (t, above)),
        remote(init_hbm.at[first], w.at[0, highs], start_send.at[4], start_recv.at[2], (t, below)),
    ]
    halos = [
        remote(u_hbm.at[0, :, last], u.at[:, lows], halo_send.at[0], halo_recv.at[0], (t, above)),
        remote(u_hbm.at[0, :, first], u.at[:, highs], halo_send.at[1], halo_recv.at[1], (t, below)),
    ]
    for copy in halos:
        copy.start()

    @pl.when(t < nt - 1)
    def _():
        for copy in starts:
            copy.start()

    @pl.when(t == 0)
    def _():
        for copy in inits:
            copy.start()

    load.wait()
    for copy in halos:
        copy.wait_recv()

    blocks = (depth + 2 * HALO - 2) // BLOCK

    def fold_block(i, carry):
        z = 1 + i * BLOCK
        forces = [force(u[k, pl.ds(z - 1, BLOCK + 2)]) for k in range(5)]
        for j in range(4):
            total = None
            for k in range(5):
                weight = h * integ[j][k] - (h * spacing[j] if j == k else 0.0)
                term = weight * forces[k]
                total = term if total is None else total + term
            corr[j, pl.ds(z, BLOCK)] = total
        return carry

    lax.fori_loop(0, blocks, fold_block, 0)

    @pl.when(t == 0)
    def _():
        local_start.wait()

    @pl.when(t > 0)
    def _():
        starts[0].wait_recv()

    starts[1].wait_recv()
    starts[2].wait_recv()

    for m in range(4):
        def sweep_block(i, carry, m=m):
            z = 1 + i * BLOCK
            here = pl.ds(z, BLOCK)
            padded = w[m, pl.ds(z - 1, BLOCK + 2)]
            now = force(padded)
            w[m + 1, here] = padded[1:-1] + (h * spacing[m]) * now + corr[m, here]
            for a in range(2):
                term = (h * (integ[2 * a][m] + integ[2 * a + 1][m])) * now
                acc[a, here] = term if m == 0 else acc[a, here] + term
            return carry

        lax.fori_loop(0, blocks, sweep_block, 0)

    write = pltpu.make_async_copy(w.at[:, own], w_out, out_sem)
    write.start()

    plane = rows * depth_c

    def last_block(i, carry):
        z = HALO + i * BLOCK
        here = pl.ds(z, BLOCK)
        padded = w[4, pl.ds(z - 1, BLOCK + 2)]
        now, end = force(padded), padded[1:-1]
        middle = w[2, here]
        outs = []
        for a in range(2):
            term = acc[a, here] + (h * (integ[2 * a][4] + integ[2 * a + 1][4])) * now
            outs.append(term + ((w[0, here] - middle) if a == 0 else (middle - end)))
        outs.append(end - u[4, here])
        for f in range(3):
            pair = outs[f].reshape(BLOCK // 2, 2, rows, cols)
            pair = pair[:, 0] + pair[:, 1]
            place = pl.multiple_of(f * plane + i * (BLOCK // 2) * rows, 8)
            restricted[pl.ds(place, BLOCK // 2 * rows), :] = pair.reshape(BLOCK // 2 * rows, cols)
        return carry

    lax.fori_loop(0, depth // BLOCK, last_block, 0)

    filled = 3 * depth_c
    pieces = []
    for x in range(rows_c):
        even = restricted[pl.ds(2 * x, filled, stride=rows), :]
        odd = restricted[pl.ds(2 * x + 1, filled, stride=rows), :]
        pieces.append((even + odd) * 0.125)
    flat = jnp.concatenate(pieces, axis=1)
    if length > filled:
        flat = jnp.concatenate([flat, jnp.zeros((length - filled, rows_c * cols), jnp.float32)], axis=0)
    for copy in tables:
        copy.wait()
    spectral = product((tab[0], tab[1]), halves(flat), ((1,), (1,)))
    send_1[...] = spectral.reshape(solvers, modes, length)

    slot = s * nt + t

    def spread(i, carry):
        other = lax.rem(me + i, solvers)

        @pl.when(other != me)
        def _():
            remote(
                send_1.at[other], recv_1.at[slot], sems.at[0], sems.at[1],
                (other // ns, lax.rem(other, ns)),
            ).start()

        return carry

    lax.fori_loop(0, solvers, spread, 0)

    def when_all(condition, body):
        if solvers == devices:
            body()
        else:
            pl.when(condition)(body)

    def bytes_wait(ref, count, sem):
        part = ref.at[pl.ds(0, count)]
        pltpu.make_async_copy(part, part, sem).wait()

    def solve():
        recv_1[slot] = send_1[me]
        bytes_wait(recv_1, devices - 1, sems.at[1])
        joined = jnp.concatenate(
            [recv_1[pl.ds(q * nt, nt)].reshape(nt * modes, length) for q in range(ns)], axis=1
        )
        spectra = product(halves(joined), (ztab[0], ztab[1]), ((1,), (0,)))
        width = inv.shape[1]
        factor = inv[pl.ds(pl.multiple_of(me * modes, 8), modes), :]
        begin = jnp.zeros((modes, width), jnp.float32)
        rows_of = []
        for n in range(nt):
            part = spectra[n * modes:(n + 1) * modes]
            middle = (begin + part[:, :width]) * factor
            finish = (middle + part[:, width:2 * width]) * factor
            rows_of.append(jnp.concatenate([begin, middle, finish], axis=1))
            begin = finish + part[:, 2 * width:]
        solved = jnp.concatenate(rows_of, axis=0)
        back = product(halves(solved), (ztab[0], ztab[1]), ((1,), (1,)))
        for q in range(ns):
            send_2[pl.ds(q * nt, nt)] = back[:, q * length:(q + 1) * length].reshape(nt, modes, length)

        def give(i, carry):
            other = lax.rem(me + i, devices)
            to_t, to_s = other // ns, lax.rem(other, ns)
            remote(
                send_2.at[to_s * nt + to_t], recv_2.at[me], sems.at[2], sems.at[3], (to_t, to_s)
            ).start()
            return carry

        lax.fori_loop(1, devices, give, 0)
        recv_2[me] = send_2[slot]
        bytes_wait(recv_2, solvers - 1, sems.at[3])

    when_all(me < solvers, solve)
    if solvers != devices:
        @pl.when(me >= solvers)
        def _():
            bytes_wait(recv_2, solvers, sems.at[3])

    delta = jnp.transpose(recv_2[...].reshape(solvers * modes, length))[:filled]
    coarse = product(halves(delta), (tab[0], tab[1]), ((1,), (0,)))
    for x in range(rows_c):
        part = coarse[:, x * cols:(x + 1) * cols]
        for side in range(2):
            up[pl.ds(2 * x + side, filled, stride=rows), :] = part
    for m in range(5):
        total = None
        for c in range(3):
            if abs(interp[m][c]) < 1e-14:
                continue
            term = up[pl.ds(c * plane, plane), :]
            if abs(interp[m][c] - 1.0) > 1e-14:
                term = interp[m][c] * term
            total = term if total is None else total + term
        timed_out[m] = total.reshape(depth_c, rows, cols)

    write.wait()
    for copy in halos:
        copy.wait_send()

    @pl.when(t < nt - 1)
    def _():
        for copy in starts:
            copy.wait_send()

    @pl.when(t == 0)
    def _():
        for copy in inits:
            copy.wait_send()

    def sent():
        bytes_wait(send_1, solvers - 1, sems.at[0])
        bytes_wait(send_2, devices - 1, sems.at[2])

    when_all(me < solvers, sent)
    if solvers != devices:
        @pl.when(me >= solvers)
        def _():
            bytes_wait(send_1, solvers, sems.at[0])


def shards(nt, ns, u_old, u_init):
    depth, rows, cols = u_init.shape
    depth_c, rows_c, cols_c = depth // 2, rows // 2, cols // 2
    whole_c = depth_c * ns
    count = rows_c * cols_c
    devices = nt * ns
    solvers = min(devices, count // 8)
    modes = count // solvers
    length = -(-3 * depth_c // 128) * 128
    extended = depth + 2 * HALO

    wide = np.repeat(hartley(cols_c), 2, axis=1)
    tab = two_parts(np.kron(hartley(rows_c), wide))
    wave = hartley(whole_c)
    ztab = np.zeros((ns, length, 3 * whole_c))
    for f in range(3):
        ztab[:, f * depth_c:(f + 1) * depth_c, f * whole_c:(f + 1) * whole_c] = wave.reshape(ns, depth_c, whole_c)
    ztab = two_parts(ztab.reshape(ns * length, 3 * whole_c))
    angle_z = 2.0 * np.cos(2.0 * np.pi * np.arange(whole_c) / whole_c)
    angle_x = 2.0 * np.cos(2.0 * np.pi * np.arange(rows_c) / rows_c)
    angle_y = 2.0 * np.cos(2.0 * np.pi * np.arange(cols_c) / cols_c)
    planar = (angle_x[:, None] + angle_y[None, :]).reshape(count)
    eigen = 0.25 * (planar[:, None] + angle_z[None, :] - 6.0)
    inv = (1.0 / (1.0 - 0.5 * step_length * diffusion * eigen)).astype(np.float32)

    anywhere = pl.BlockSpec(memory_space=pl.ANY)
    f32 = jnp.float32
    w, timed = pl.pallas_call(
        functools.partial(kernel, nt, ns, solvers),
        out_shape=(
            jax.ShapeDtypeStruct((5, depth, rows, cols), f32),
            jax.ShapeDtypeStruct((5, depth_c, rows, cols), f32),
        ),
        in_specs=[anywhere] * 5,
        out_specs=(anywhere, pl.BlockSpec(memory_space=pltpu.VMEM)),
        scratch_shapes=[
            pltpu.VMEM((5, extended, rows, cols), f32),
            pltpu.VMEM((5, extended, rows, cols), f32),
            pltpu.VMEM((4, extended, rows, cols), f32),
            pltpu.VMEM((2, extended, rows, cols), f32),
            pltpu.VMEM((3 * depth_c * rows, cols), f32),
            pltpu.VMEM(tab.shape, jnp.bfloat16),
            pltpu.VMEM(ztab.shape, jnp.bfloat16),
            pltpu.VMEM(inv.shape, f32),
            pltpu.VMEM((solvers, modes, length), f32),
            pltpu.VMEM((devices, modes, length), f32),
            pltpu.VMEM((devices, modes, length), f32),
            pltpu.VMEM((solvers, modes, length), f32),
            pltpu.VMEM((3 * depth_c * rows, cols), f32),
            pltpu.SemaphoreType.DMA,
            pltpu.SemaphoreType.DMA((3,)),
            pltpu.SemaphoreType.DMA,
            pltpu.SemaphoreType.DMA,
            pltpu.SemaphoreType.DMA((2,)),
            pltpu.SemaphoreType.DMA((2,)),
            pltpu.SemaphoreType.DMA((5,)),
            pltpu.SemaphoreType.DMA((3,)),
            pltpu.SemaphoreType.DMA((4,)),
        ],
        compiler_params=pltpu.CompilerParams(
            collective_id=0, has_side_effects=True, vmem_limit_bytes=48 * 1024 * 1024
        ),
    )(u_old, u_init, tab, ztab, inv)
    result = w.reshape(5, depth_c, 2, rows, cols) + timed[:, :, None]
    return result.reshape(1, 5, depth, rows, cols)


def solution(mesh):
    return jax.shard_map(
        functools.partial(shards, mesh.shape["tm"], mesh.shape["space"]),
        mesh=mesh,
        in_specs=(P("tm", None, "space", None, None), P("space", None, None)),
        out_specs=P("tm", None, "space", None, None),
        check_vma=False,
    )
```

time: 497 us -> 56.7 us (0.11); the launches traced: 489 us -> 56.4 us
  local copies, waits for them, and re-layouts: 264 us -> 6.44 us
  other arithmetic: 111 us -> 1.83 us
  blocking collectives: 68.6 us -> 0 us
  Pallas kernels: 0 us -> 48.1 us
  matrix products: 17.7 us -> 0 us
  starting transfers between devices: 16.5 us -> 0 us
  waiting for transfers between devices: 10.1 us -> 0 us
    reshape x6 -> x0, local copies, waits for them, and re-layouts: 145 us -> none  [the longest x4 140 us: restrict(): field.reshape(depth // 2, 2, rows // 2, 2, cols // 2, 2)]
    reduce_sum x6 -> x0, other arithmetic: 74.7 us -> none  [restrict(): return field.reshape(depth // 2, 2, rows // 2, 2, cols // 2, 2).mean(axis...]
    add x2 -> x1, local copies, waits for them, and re-layouts: 69.7 us -> 0.21 us  [shards(): result = w.reshape(5, depth_c, 2, rows, cols) + timed[:, :, None]]
    all_gather x2 -> x0, blocking collectives: 48.3 us -> none  [entering(): gathered = jax.tree.map(lambda a: lax.all_gather(a, axis), part)]
    pallas_call x0 -> x1, Pallas kernels: none -> 48.1 us  [shards(): pl.pallas_call(functools.partial(kernel, nt, ns, solvers), out_shape=(jax...]
    slice x31 -> x0, local copies, waits for them, and re-layouts: 29.6 us -> none  [the longest x12 16.2 us: local_force(): near = near + jnp.roll(field, 1, 3) + jnp.roll(field, -1, 3)]
    all_to_all x1 -> x0, blocking collectives: 20.3 us -> none  [shards(): lax.all_to_all(planar, 'space', split_axis=1, concat_axis=2, tiled=True)]
    dot_general x7 -> x0, matrix products: 17.7 us -> none  [the longest x1 5.45 us: shards(): jnp.einsum('jk,kzxy->jzxy', integ, fold, precision=highest)]
  transfers between devices with their start and end apart: 14 -> 0, of which waited for: 4 -> 0; matrix products, arithmetic and copies ran while one was open for 25% -> 0% of each run, Pallas kernels for 0% -> 0%
where the time goes in v1:
time: 56.7 us; the launch traced here: 56.4 us
  Pallas kernels  48.1 us (85%)
  local copies, waits for them, and re-layouts  6.44 us (11%)
  other arithmetic  1.83 us (3%)
    pallas_call x1, Pallas kernels, shards(): pl.pallas_call(functools.partial(kernel, nt, ns, solvers), out_shape=(jax...  48.1 us
    unnamed x10, local copies, waits for them, and re-layouts  6.23 us
    add x1, other arithmetic, shards(): result = w.reshape(5, depth_c, 2, rows, cols) + timed[:, :, None]  1.83 us

profile of v1, /device:TPU:25, one launch (start us, length us, event | category | flops | bytes accessed | tf_op | source)
XLA Modules:
  0.0 56.4 jit_solution(17919757321694261778)
XLA Ops:
  0.0 0.0 copy-start
  0.0 1.6 %copy-done = bf16[2,512,1024]{2,1,0:T(8,128)(2,1)S(1)} copy-done((bf16[2,512,1024]{2,1,0:T(8,128)(2,1)S(1)}, bf16[2,512,1024]{2,1,0:T(8,128)(2,1)}, u32[]{:S(2)}) %copy-start) | copy-done | bytes 2097176
  1.6 0.0 copy-start.1
  1.6 1.1 %copy-done.1 = bf16[2,512,384]{2,1,0:T(8,128)(2,1)S(1)} copy-done((bf16[2,512,384]{2,1,0:T(8,128)(2,1)S(1)}, bf16[2,512,384]{2,1,0:T(8,128)(2,1)}, u32[]{:S(2)}) %copy-start.1) | copy-done | bytes 786456
  2.7 0.0 copy-start.2
  2.7 1.0 %copy-done.2 = f32[64,16,128]{2,1,0:T(8,128)S(1)} copy-done((f32[64,16,128]{2,1,0:T(8,128)S(1)}, f32[64,16,128]{2,1,0:T(8,128)}, u32[]{:S(2)}) %copy-start.2) | copy-done | bytes 524312
  3.8 0.0 copy-start.3
  3.8 0.9 %copy-done.3 = f32[512,128]{1,0:T(8,128)S(1)} copy-done((f32[512,128]{1,0:T(8,128)S(1)}, f32[512,128]{1,0:T(8,128)}, u32[]{:S(2)}) %copy-start.3) | copy-done | bytes 262168
  4.7 48.1 %shard_map.55 = (f32[5,64,16,128]{3,2,1,0:T(8,128)}, f32[5,32,16,128]{3,2,1,0:T(8,128)S(1)}) custom-call(f32[1,5,64,16,128]{4,3,2,1,0:T(8,128)} %u_hbm.1, f32[64,16,128]{2,1,0:T(8,128)S(1)} %copy-done.2, bf16[2,512,1024]{2,1,0:T(8,128)(2,1)S(1)} %copy-done, bf16[2,512,384]{2,1,0:T(8,128)(2,1)S(1)} %copy-done.1, f32[512,128]{1,0:T(8,128)S(1)} %copy-done.3), custom_call_target="tpu_custom_call" | custom-call | tf_op jit(solution)/shard_map/pallas_call | solution.py:402
  52.8 0.0 copy-start.4
  52.9 0.2 add.14
  53.1 1.5 %copy-done.4 = f32[5,64,16,128]{3,2,1,0:T(8,128)S(1)} copy-done((f32[5,64,16,128]{3,2,1,0:T(8,128)S(1)}, f32[5,64,16,128]{3,2,1,0:T(8,128)}, u32[]{:S(2)}) %copy-start.4) | copy-done | bytes 2621464
  54.6 1.8 %add_bitcast_fusion = f32[1,5,64,16,128]{4,3,2,1,0:T(8,128)} fusion(f32[5,64,16,128]{3,2,1,0:T(8,128)S(1)} %copy-done.4, f32[5,64,16,128]{3,2,1,0:T(8,128)S(1)} %bitcast.3), kind=kLoop, calls=%fused_computation | loop fusion | flops 655360 | bytes 7864320 | tf_op jit(solution)/shard_map/add | solution.py:438
Async XLA Ops:
  0.0 1.6 %copy-start = (bf16[2,512,1024]{2,1,0:T(8,128)(2,1)S(1)}, bf16[2,512,1024]{2,1,0:T(8,128)(2,1)}, u32[]{:S(2)}) copy-start(bf16[2,512,1024]{2,1,0:T(8,128)(2,1)} %constant.6.clone.tab_hbm) | copy-start | bytes 6291460
  1.6 1.1 %copy-start.1 = (bf16[2,512,384]{2,1,0:T(8,128)(2,1)S(1)}, bf16[2,512,384]{2,1,0:T(8,128)(2,1)}, u32[]{:S(2)}) copy-start(bf16[2,512,384]{2,1,0:T(8,128)(2,1)} %constant.7.clone.ztab_hbm) | copy-start | bytes 2359300
  2.7 1.0 %copy-start.2 = (f32[64,16,128]{2,1,0:T(8,128)S(1)}, f32[64,16,128]{2,1,0:T(8,128)}, u32[]{:S(2)}) copy-start(f32[64,16,128]{2,1,0:T(8,128)} %init_hbm.1) | copy-start | bytes 1572868
  3.8 0.9 %copy-start.3 = (f32[512,128]{1,0:T(8,128)S(1)}, f32[512,128]{1,0:T(8,128)}, u32[]{:S(2)}) copy-start(f32[512,128]{1,0:T(8,128)} %constant.8.clone.inv_hbm) | copy-start | bytes 786436
  52.8 1.7 %copy-start.4 = (f32[5,64,16,128]{3,2,1,0:T(8,128)S(1)}, f32[5,64,16,128]{3,2,1,0:T(8,128)}, u32[]{:S(2)}) copy-start(f32[5,64,16,128]{3,2,1,0:T(8,128)} %get-tuple-element.7) | copy-start | bytes 7864324

commit v2 on v1

--- a/solution.py
+++ b/solution.py
@@ -99,11 +99,11 @@
 def kernel(
     nt, ns, solvers,
     u_hbm, init_hbm, tab_hbm, ztab_hbm, inv_hbm,
-    w_out, timed_out,
+    out,
     u, w, corr, acc, restricted, tab, ztab, inv,
     send_1, recv_1, send_2, recv_2, up,
-    load_sem, table_sem, out_sem, start_sem, halo_send, halo_recv, start_send, start_recv,
-    sems,
+    load_sem, table_sem, start_sem, halo_send, halo_recv, start_send, start_recv,
+    sems, known_sem,
 ):
     integ, spacing, interp = node_tables()
     h = step_length
@@ -119,14 +119,23 @@
 
     barrier = pltpu.get_barrier_semaphore()
 
-    def greet(i, carry):
-        other = lax.rem(me + i, devices)
+    def signal_along(sem, step):
+        @pl.when(t + step < nt)
+        def _():
+            pl.semaphore_signal(sem, inc=1, device_id=(t + step, s), device_id_type=MESH)
+
+        @pl.when(t >= step)
+        def _():
+            pl.semaphore_signal(sem, inc=1, device_id=(t - step, s), device_id_type=MESH)
+
+    def sides(step):
+        return jnp.where(t + step < nt, 1, 0) + jnp.where(t >= step, 1, 0)
+
+    signal_along(barrier, 1)
+    for i in range(1, ns):
         pl.semaphore_signal(
-            barrier, inc=1, device_id=(other // ns, lax.rem(other, ns)), device_id_type=MESH
+            barrier, inc=1, device_id=(t, lax.rem(s + i, ns)), device_id_type=MESH
         )
-        return carry
-
-    lax.fori_loop(1, devices, greet, 0)
     load = pltpu.make_async_copy(u_hbm.at[0], u.at[:, own], load_sem)
     load.start()
     tables = [
@@ -141,7 +150,7 @@
     def _():
         local_start.start()
 
-    pl.semaphore_wait(barrier, devices - 1)
+    pl.semaphore_wait(barrier, ns - 1 + sides(1))
 
     lows, highs = pl.ds(0, HALO), pl.ds(HALO + depth, HALO)
     first, last = pl.ds(0, HALO), pl.ds(depth - HALO, HALO)
@@ -154,32 +163,46 @@
 
     after = jnp.minimum(t + 1, nt - 1)
     node = u_hbm.at[0, 4]
+    cuts = [(0, HALO), (depth - HALO, HALO), (HALO, depth - 2 * HALO)]
     starts = [
-        remote(node, w.at[0, own], start_send.at[0], start_recv.at[0], (after, s)),
-        remote(node.at[last], w.at[0, lows], start_send.at[1], start_recv.at[1], (after, above)),
-        remote(node.at[first], w.at[0, highs], start_send.at[2], start_recv.at[2], (after, below)),
+        remote(
+            node.at[pl.ds(begin, size)], w.at[0, pl.ds(HALO + begin, size)],
+            start_send.at[i], start_recv.at[i], (after, s),
+        )
+        for i, (begin, size) in enumerate(cuts)
     ]
-    inits = [
-        remote(init_hbm.at[last], w.at[0, lows], start_send.at[3], start_recv.at[1], (t, above)),
-        remote(init_hbm.at[first], w.at[0, highs], start_send.at[4], start_recv.at[2], (t, below)),
-    ]
+
+    def edges(source, shift):
+        return [
+            remote(
+                source.at[pl.ds(shift + depth - HALO, HALO)], w.at[0, lows],
+                start_send.at[3], start_recv.at[3], (t, above),
+            ),
+            remote(
+                source.at[pl.ds(shift, HALO)], w.at[0, highs],
+                start_send.at[4], start_recv.at[4], (t, below),
+            ),
+        ]
+
+    inits, passed = edges(init_hbm, 0), edges(w.at[0], HALO)
     halos = [
         remote(u_hbm.at[0, :, last], u.at[:, lows], halo_send.at[0], halo_recv.at[0], (t, above)),
         remote(u_hbm.at[0, :, first], u.at[:, highs], halo_send.at[1], halo_recv.at[1], (t, below)),
     ]
+    @pl.when(t < nt - 1)
+    def _():
+        for copy in starts:
+            copy.start()
+
     for copy in halos:
         copy.start()
 
-    @pl.when(t < nt - 1)
-    def _():
-        for copy in starts:
-            copy.start()
-
     @pl.when(t == 0)
     def _():
         for copy in inits:
             copy.start()
 
+    signal_along(known_sem.at[0], 1)
     load.wait()
     for copy in halos:
         copy.wait_recv()
@@ -206,10 +229,22 @@
 
     @pl.when(t > 0)
     def _():
+        starts[1].wait_recv()
+        passed[0].start()
         starts[0].wait_recv()
-
-    starts[1].wait_recv()
-    starts[2].wait_recv()
+        passed[1].start()
+
+    for i in range(known_sem.shape[0]):
+        if i > 0:
+            signal_along(known_sem.at[i], 2 ** i)
+        pl.semaphore_wait(known_sem.at[i], sides(2 ** i))
+
+    @pl.when(t > 0)
+    def _():
+        starts[2].wait_recv()
+
+    for copy in inits:
+        copy.wait_recv()
 
     for m in range(4):
         def sweep_block(i, carry, m=m):
@@ -224,9 +259,6 @@
             return carry
 
         lax.fori_loop(0, blocks, sweep_block, 0)
-
-    write = pltpu.make_async_copy(w.at[:, own], w_out, out_sem)
-    write.start()
 
     plane = rows * depth_c
 
@@ -336,18 +368,29 @@
         part = coarse[:, x * cols:(x + 1) * cols]
         for side in range(2):
             up[pl.ds(2 * x + side, filled, stride=rows), :] = part
-    for m in range(5):
-        total = None
-        for c in range(3):
-            if abs(interp[m][c]) < 1e-14:
-                continue
-            term = up[pl.ds(c * plane, plane), :]
-            if abs(interp[m][c] - 1.0) > 1e-14:
-                term = interp[m][c] * term
-            total = term if total is None else total + term
-        timed_out[m] = total.reshape(depth_c, rows, cols)
-
-    write.wait()
+
+    def add_block(i, carry):
+        fields = [
+            up[pl.ds(pl.multiple_of(c * plane + i * (BLOCK // 2) * rows, 8), BLOCK // 2 * rows), :]
+            for c in range(3)
+        ]
+        for m in range(5):
+            total = None
+            for c in range(3):
+                if abs(interp[m][c]) < 1e-14:
+                    continue
+                term = fields[c]
+                if abs(interp[m][c] - 1.0) > 1e-14:
+                    term = interp[m][c] * term
+                total = term if total is None else total + term
+            total = total.reshape(BLOCK // 2, 1, rows, cols)
+            total = jnp.broadcast_to(total, (BLOCK // 2, 2, rows, cols)).reshape(BLOCK, rows, cols)
+            z = i * BLOCK
+            out[0, m, pl.ds(z, BLOCK)] = w[m, pl.ds(HALO + z, BLOCK)] + total
+        return carry
+
+    lax.fori_loop(0, depth // BLOCK, add_block, 0)
+
     for copy in halos:
         copy.wait_send()
 
@@ -356,10 +399,8 @@
         for copy in starts:
             copy.wait_send()
 
-    @pl.when(t == 0)
-    def _():
-        for copy in inits:
-            copy.wait_send()
+    for copy in inits:
+        copy.wait_send()
 
     def sent():
         bytes_wait(send_1, solvers - 1, sems.at[0])
@@ -382,6 +423,7 @@
     modes = count // solvers
     length = -(-3 * depth_c // 128) * 128
     extended = depth + 2 * HALO
+    rounds = max(1, (nt - 1).bit_length())
 
     wide = np.repeat(hartley(cols_c), 2, axis=1)
     tab = two_parts(np.kron(hartley(rows_c), wide))
@@ -397,16 +439,12 @@
     eigen = 0.25 * (planar[:, None] + angle_z[None, :] - 6.0)
     inv = (1.0 / (1.0 - 0.5 * step_length * diffusion * eigen)).astype(np.float32)
 
-    anywhere = pl.BlockSpec(memory_space=pl.ANY)
     f32 = jnp.float32
-    w, timed = pl.pallas_call(
+    return pl.pallas_call(
         functools.partial(kernel, nt, ns, solvers),
-        out_shape=(
-            jax.ShapeDtypeStruct((5, depth, rows, cols), f32),
-            jax.ShapeDtypeStruct((5, depth_c, rows, cols), f32),
-        ),
-        in_specs=[anywhere] * 5,
-        out_specs=(anywhere, pl.BlockSpec(memory_space=pltpu.VMEM)),
+        out_shape=jax.ShapeDtypeStruct((1, 5, depth, rows, cols), f32),
+        in_specs=[pl.BlockSpec(memory_space=pltpu.HBM)] * 5,
+        out_specs=pl.BlockSpec(memory_space=pltpu.VMEM),
         scratch_shapes=[
             pltpu.VMEM((5, extended, rows, cols), f32),
             pltpu.VMEM((5, extended, rows, cols), f32),
@@ -424,19 +462,17 @@
             pltpu.SemaphoreType.DMA,
             pltpu.SemaphoreType.DMA((3,)),
             pltpu.SemaphoreType.DMA,
-            pltpu.SemaphoreType.DMA,
             pltpu.SemaphoreType.DMA((2,)),
             pltpu.SemaphoreType.DMA((2,)),
             pltpu.SemaphoreType.DMA((5,)),
-            pltpu.SemaphoreType.DMA((3,)),
+            pltpu.SemaphoreType.DMA((5,)),
             pltpu.SemaphoreType.DMA((4,)),
+            pltpu.SemaphoreType.REGULAR((rounds,)),
         ],
         compiler_params=pltpu.CompilerParams(
-            collective_id=0, has_side_effects=True, vmem_limit_bytes=48 * 1024 * 1024
+            collective_id=0, has_side_effects=True, vmem_limit_bytes=62000000
         ),
     )(u_old, u_init, tab, ztab, inv)
-    result = w.reshape(5, depth_c, 2, rows, cols) + timed[:, :, None]
-    return result.reshape(1, 5, depth, rows, cols)
 
 
 def solution(mesh):

time: 56.7 us -> 49.5 us (0.87)
  local copies, waits for them, and re-layouts: 6.44 us -> 3.52 us
  Pallas kernels: 48.1 us -> 45.8 us
  other arithmetic: 1.83 us -> 0 us
    unnamed x10 -> x1, local copies, waits for them, and re-layouts: 6.23 us -> 3.52 us
    pallas_call x1, Pallas kernels: 48.1 us -> 45.8 us  [shards(): pl.pallas_call(functools.partial(kernel, nt, ns, solvers), out_shape=jax....]
    add x1 -> x0, other arithmetic: 1.83 us -> none  [shards(): result = w.reshape(5, depth_c, 2, rows, cols) + timed[:, :, None]]
where the time goes in v2:
time: 49.5 us; the launch traced here: 49.3 us
  Pallas kernels  45.8 us (93%)
  local copies, waits for them, and re-layouts  3.52 us (7%)
    pallas_call x1, Pallas kernels, shards(): pl.pallas_call(functools.partial(kernel, nt, ns, solvers), out_shape=jax....  45.8 us
    unnamed x1, local copies, waits for them, and re-layouts  3.52 us

profile of v2, /device:TPU:25, one launch (start us, length us, event | category | flops | bytes accessed | tf_op | source)
XLA Modules:
  0.0 49.3 jit_solution(7509000753272284518)
XLA Ops:
  0.0 45.8 %shard_map.55 = f32[1,5,64,16,128]{4,3,2,1,0:T(8,128)} custom-call(f32[1,5,64,16,128]{4,3,2,1,0:T(8,128)} %u_hbm.1, f32[64,16,128]{2,1,0:T(8,128)} %init_hbm.1, bf16[2,512,1024]{2,1,0:T(8,128)(2,1)} %constant.6.clone.tab_hbm, bf16[2,512,384]{2,1,0:T(8,128)(2,1)} %constant.7.clone.ztab_hbm, f32[512,128]{1,0:T(8,128)} %constant.8.clone.inv_hbm), custom_call_target="tpu_custom_call" | custom-call | tf_op jit(solution)/shard_map/pallas_call | solution.py:443
  45.8 3.5 %copy.7 = f32[1,5,64,16,128]{4,3,2,1,0:T(8,128)} copy(f32[1,5,64,16,128]{4,3,2,1,0:T(8,128)} %shard_map.55) | data formatting | bytes 5242880
